TPU v7x, 32 devices: a whole 2x2x4 slice. The times are simulated.
32 devices in a mesh: fsdp: 4 (over y, x), seq: 8 (over z, core).
Axes of the slice: x: 2, y: 2, z: 4, core: 2. Of those that a mesh axis runs over, the one named last changes fastest.
Arguments:
- images: bfloat16 [32, 1024, 1152], P('fsdp', 'seq'), may hold values from -8 to 8
- lengths: int32 [32], P('fsdp'), may hold values from 256 to 1024
- ln1_gain: bfloat16 [1152], P('fsdp'), may hold values from 0.099609375 to 1.8984375
- ln1_bias: bfloat16 [1152], P('fsdp'), may hold values from -3 to 3
- w_qkv: bfloat16 [1152, 3456], P('fsdp'), may hold values from -1 to 1
- qv_bias: bfloat16 [2, 1152], P(None, 'fsdp'), may hold values from -3 to 3
- w_out: bfloat16 [1152, 1152], P('fsdp'), may hold values from -0.75 to 0.75
- out_bias: bfloat16 [1152], P('fsdp'), may hold values from -3 to 3
- ln2_gain: bfloat16 [1152], P('fsdp'), may hold values from 0.099609375 to 1.8984375
- ln2_bias: bfloat16 [1152], P('fsdp'), may hold values from -3 to 3
- w_up: bfloat16 [1152, 4304], P('fsdp'), may hold values from -0.1875 to 0.1875
- up_bias: bfloat16 [4304], P('fsdp'), may hold values from -3 to 3
- w_down: bfloat16 [4304, 1152], P(None, 'fsdp'), may hold values from -0.09375 to 0.09375
- down_bias: bfloat16 [1152], P('fsdp'), may hold values from -3 to 3
- cotangent: bfloat16 [32, 1024, 1152], P('fsdp', 'seq'), may hold values from -6 to 6
Outputs:
- layer_out: bfloat16 [32, 1024, 1152], P('fsdp', 'seq')
- grad_images: bfloat16 [32, 1024, 1152], P('fsdp', 'seq')
- grad_ln1_gain: float32 [1152], P('fsdp')
- grad_ln1_bias: float32 [1152], P('fsdp')
- grad_w_qkv: float32 [1152, 3456], P('fsdp')
- grad_qv_bias: float32 [2, 1152], P(None, 'fsdp')
- grad_w_out: float32 [1152, 1152], P('fsdp')
- grad_out_bias: float32 [1152], P('fsdp')
- grad_ln2_gain: float32 [1152], P('fsdp')
- grad_ln2_bias: float32 [1152], P('fsdp')
- grad_w_up: float32 [1152, 4304], P('fsdp')
- grad_up_bias: float32 [4304], P('fsdp')
- grad_w_down: float32 [4304, 1152], P(None, 'fsdp')
- grad_down_bias: float32 [1152], P('fsdp')
All inputs are finite; a program needn't handle non-finite values.
Results may differ from a plain program's by a relative error of at most 0.017.
Values may be sent and summed in bfloat16 or wider, within the bound.
A program may use at most 256 MiB of HBM per device.

v0:
```python
import jax
import jax.numpy as jnp
from jax import lax
from jax.sharding import PartitionSpec as P

H = 16
HD = 72
epsilon = 1e-06
wide_block = 1024


def for_sending(shard):

    def short(part):
        return part.astype(jnp.bfloat16) if part.dtype == jnp.float32 else part

    return jax.tree.map(short, shard)


def normalize(field, gain_vec, bias_vec):
    center_mean = jnp.mean(field, -1, keepdims=True)
    centered = field - center_mean
    variance = jnp.mean(centered * centered, -1, keepdims=True)
    return centered * lax.rsqrt(variance + epsilon) * gain_vec + bias_vec


def gelu_tanh(field):
    return jax.nn.gelu(field, approximate=True)


def attend_item(queries, keys_all, values, length_one):
    length_all = keys_all.shape[1]
    block_rows = min(wide_block, length_all)
    visible = (jnp.arange(length_all) < length_one)[None, :]
    pieces = []
    log_sums = []
    for offset in range(0, length_all, block_rows):
        scores = jnp.einsum(
            "dq,dk->qk",
            queries[:, offset : offset + block_rows],
            keys_all,
            preferred_element_type=jnp.float32,
        )
        scores = jnp.where(visible, scores, -1e30)
        row_max = jnp.max(scores, -1, keepdims=True)
        exponents = jnp.exp(scores - row_max)
        denominator = jnp.sum(exponents, -1, keepdims=True)
        softmax_low = (exponents / denominator).astype(jnp.bfloat16)
        pieces.append(
            jnp.einsum("qk,dk->dq", softmax_low, values, preferred_element_type=jnp.float32)
        )
        log_sums.append(row_max[:, 0] + jnp.log(denominator[:, 0]))
    return (jnp.concatenate(pieces, 1).astype(jnp.bfloat16), jnp.concatenate(log_sums, 0))


def attend_back(queries, keys_all, values, length_one, log_sum, grad_mixed):
    length_all = keys_all.shape[1]
    block_rows = min(wide_block, length_all)
    visible = (jnp.arange(length_all) < length_one)[None, :]
    grad_keys = jnp.zeros(keys_all.shape, jnp.float32)
    grad_values = jnp.zeros(values.shape, jnp.float32)
    grad_pieces = []
    for offset in range(0, length_all, block_rows):
        query_rows = queries[:, offset : offset + block_rows]
        grad_rows = grad_mixed[:, offset : offset + block_rows]
        scores = jnp.einsum("dq,dk->qk", query_rows, keys_all, preferred_element_type=jnp.float32)
        scores = jnp.where(visible, scores, -1e30)
        softmax_out = jnp.exp(scores - log_sum[offset : offset + block_rows, None])
        grad_soft = jnp.einsum("dq,dk->qk", grad_rows, values, preferred_element_type=jnp.float32)
        row_dot = jnp.sum(softmax_out * grad_soft, -1, keepdims=True)
        grad_scores = (softmax_out * (grad_soft - row_dot)).astype(jnp.bfloat16)
        grad_pieces.append(
            jnp.einsum("qk,dk->dq", grad_scores, keys_all, preferred_element_type=jnp.float32)
        )
        grad_keys = grad_keys + jnp.einsum(
            "qk,dq->dk", grad_scores, query_rows, preferred_element_type=jnp.float32
        )
        grad_values = grad_values + jnp.einsum(
            "qk,dq->dk",
            softmax_out.astype(jnp.bfloat16),
            grad_rows,
            preferred_element_type=jnp.float32,
        )
    return (
        jnp.concatenate(grad_pieces, 1).astype(jnp.bfloat16),
        grad_keys.astype(jnp.bfloat16),
        grad_values.astype(jnp.bfloat16),
    )


def on_device(
    images,
    lengths,
    ln1_gain,
    ln1_bias,
    w_qkv,
    qv_bias,
    w_out,
    out_bias,
    ln2_gain,
    ln2_bias,
    w_up,
    up_bias,
    w_down,
    down_bias,
    cotangent,
):
    image_count, token_count, width_all = images.shape
    head_scale = HD ** (-0.5)
    gain_first, bias_first, qkv_full, qv_full, out_full, outb_full = (
        lax.all_gather(ln1_gain, "fsdp", axis=0, tiled=True),
        lax.all_gather(ln1_bias, "fsdp", axis=0, tiled=True),
        lax.all_gather(w_qkv, "fsdp", axis=0, tiled=True),
        lax.all_gather(qv_bias, "fsdp", axis=1, tiled=True),
        lax.all_gather(w_out, "fsdp", axis=0, tiled=True),
        lax.all_gather(out_bias, "fsdp", axis=0, tiled=True),
    )
    inputs_all = images.astype(jnp.float32)
    normed_first, norm_first_back = jax.vjp(
        normalize, inputs_all, gain_first.astype(jnp.float32), bias_first.astype(jnp.float32)
    )
    normed_attn = normed_first.astype(jnp.bfloat16)
    qkv_split = qkv_full.reshape(width_all, 3, H, HD)
    projected = jnp.einsum(
        "itd,dahe->ahiet", normed_attn, qkv_split, preferred_element_type=jnp.float32
    )
    shift_pair = qv_full.astype(jnp.float32).reshape(2, H, HD)
    queries = (projected[0] + shift_pair[0][:, None, :, None]) * head_scale
    values = projected[2] + shift_pair[1][:, None, :, None]
    stacked = jnp.stack([queries, projected[1], values]).astype(jnp.bfloat16)
    head_view = lax.all_to_all(stacked, "seq", split_axis=1, concat_axis=4, tiled=True)
    local_heads = head_view.shape[1]
    item_count = local_heads * image_count
    query_items = head_view[0].reshape(item_count, HD, -1)
    key_items = head_view[1].reshape(item_count, HD, -1)
    value_items = head_view[2].reshape(item_count, HD, -1)
    item_lengths = jnp.tile(lengths, local_heads)
    mixed_items, log_sums = lax.map(
        lambda packed: attend_item(*packed), (query_items, key_items, value_items, item_lengths)
    )
    mixed_tokens = lax.all_to_all(
        for_sending(mixed_items.reshape(local_heads, image_count, HD, -1)),
        "seq",
        split_axis=3,
        concat_axis=0,
        tiled=True,
    )
    out_split = out_full.reshape(H, HD, width_all)
    residual = (
        inputs_all
        + jnp.einsum("hiet,hed->itd", mixed_tokens, out_split, preferred_element_type=jnp.float32)
        + outb_full.astype(jnp.float32)
    )
    gain_second, bias_second, up_full, upb_full, down_full, downb_full = (
        lax.all_gather(ln2_gain, "fsdp", axis=0, tiled=True),
        lax.all_gather(ln2_bias, "fsdp", axis=0, tiled=True),
        lax.all_gather(w_up, "fsdp", axis=0, tiled=True),
        lax.all_gather(up_bias, "fsdp", axis=0, tiled=True),
        lax.all_gather(w_down, "fsdp", axis=1, tiled=True),
        lax.all_gather(down_bias, "fsdp", axis=0, tiled=True),
    )
    normed_second, norm_second_back = jax.vjp(
        normalize, residual, gain_second.astype(jnp.float32), bias_second.astype(jnp.float32)
    )
    normed_mlp = normed_second.astype(jnp.bfloat16)
    pre_act = jnp.einsum(
        "itd,df->itf", normed_mlp, up_full, preferred_element_type=jnp.float32
    ) + upb_full.astype(jnp.float32)
    activation, gelu_back = jax.vjp(gelu_tanh, pre_act)
    activation = activation.astype(jnp.bfloat16)
    output_all = (
        residual
        + jnp.einsum("itf,fd->itd", activation, down_full, preferred_element_type=jnp.float32)
        + downb_full.astype(jnp.float32)
    )
    layer_out = output_all.astype(jnp.bfloat16)
    qkv_back, out_back = (
        lax.all_gather(w_qkv, "fsdp", axis=0, tiled=True),
        lax.all_gather(w_out, "fsdp", axis=0, tiled=True),
    )
    up_back, down_back = (
        lax.all_gather(w_up, "fsdp", axis=0, tiled=True),
        lax.all_gather(w_down, "fsdp", axis=1, tiled=True),
    )
    grad_down = jnp.einsum("itf,itd->fd", activation, cotangent, preferred_element_type=jnp.float32)
    grad_downb = jnp.sum(cotangent, axis=(0, 1), dtype=jnp.float32)
    grad_act = jnp.einsum("itd,fd->itf", cotangent, down_back, preferred_element_type=jnp.float32)
    (grad_pre,) = gelu_back(grad_act)
    grad_pre = grad_pre.astype(jnp.bfloat16)
    grad_up = jnp.einsum("itd,itf->df", normed_mlp, grad_pre, preferred_element_type=jnp.float32)
    grad_upb = jnp.sum(grad_pre, axis=(0, 1), dtype=jnp.float32)
    grad_normed_mlp = jnp.einsum(
        "itf,df->itd", grad_pre, up_back, preferred_element_type=jnp.float32
    )
    grad_resid_norm, grad_gain_second, grad_bias_second = norm_second_back(grad_normed_mlp)
    grad_residual = cotangent.astype(jnp.float32) + grad_resid_norm
    grad_branch = grad_residual.astype(jnp.bfloat16)
    grad_outw = jnp.einsum(
        "hiet,itd->hed", mixed_tokens, grad_branch, preferred_element_type=jnp.float32
    ).reshape(width_all, width_all)
    grad_outb = jnp.sum(grad_branch, axis=(0, 1), dtype=jnp.float32)
    out_back_split = out_back.reshape(H, HD, width_all)
    grad_mixed = jnp.einsum(
        "itd,hed->hiet", grad_branch, out_back_split, preferred_element_type=jnp.float32
    ).astype(jnp.bfloat16)
    grad_head_view = lax.all_to_all(grad_mixed, "seq", split_axis=0, concat_axis=3, tiled=True)
    grad_items = grad_head_view.reshape(item_count, HD, -1)
    grad_q, grad_k, grad_v = lax.map(
        lambda packed: attend_back(*packed),
        (query_items, key_items, value_items, item_lengths, log_sums, grad_items),
    )
    grad_stack = jnp.stack([grad_q, grad_k, grad_v]).reshape(3, local_heads, image_count, HD, -1)
    grad_projected = lax.all_to_all(
        for_sending(grad_stack), "seq", split_axis=4, concat_axis=1, tiled=True
    ).astype(grad_stack.dtype)
    column_scales = jnp.array([head_scale, 1.0, 1.0], jnp.float32)
    grad_qkv = (
        jnp.einsum(
            "itd,ahiet->dahe", normed_attn, grad_projected, preferred_element_type=jnp.float32
        )
        * column_scales[None, :, None, None]
    ).reshape(width_all, 3 * width_all)
    shift_sums = jnp.sum(grad_projected, axis=(2, 4), dtype=jnp.float32)
    grad_qvb = jnp.stack([shift_sums[0] * head_scale, shift_sums[2]]).reshape(2, width_all)
    qkv_back_split = qkv_back.reshape(width_all, 3, H, HD)
    grad_normed_attn = head_scale * jnp.einsum(
        "hiet,dhe->itd", grad_projected[0], qkv_back_split[:, 0], preferred_element_type=jnp.float32
    )
    grad_normed_attn = grad_normed_attn + jnp.einsum(
        "ahiet,dahe->itd",
        grad_projected[1:],
        qkv_back_split[:, 1:],
        preferred_element_type=jnp.float32,
    )
    grad_input_norm, grad_gain_first, grad_bias_first = norm_first_back(grad_normed_attn)
    grad_images = (grad_residual + grad_input_norm).astype(jnp.bfloat16)
    (
        part_gone,
        part_bone,
        part_qkv,
        part_qvb,
        part_outw,
        part_outb,
        part_gtwo,
        part_btwo,
        part_up,
        part_upb,
        part_down,
        part_downb,
    ) = (
        lax.psum_scatter(
            grad_gain_first.astype(jnp.bfloat16), "fsdp", scatter_dimension=0, tiled=True
        ).astype(jnp.float32),
        lax.psum_scatter(
            grad_bias_first.astype(jnp.bfloat16), "fsdp", scatter_dimension=0, tiled=True
        ).astype(jnp.float32),
        lax.psum_scatter(
            grad_qkv.astype(jnp.bfloat16), "fsdp", scatter_dimension=0, tiled=True
        ).astype(jnp.float32),
        lax.psum_scatter(
            grad_qvb.astype(jnp.bfloat16), "fsdp", scatter_dimension=1, tiled=True
        ).astype(jnp.float32),
        lax.psum_scatter(
            grad_outw.astype(jnp.bfloat16), "fsdp", scatter_dimension=0, tiled=True
        ).astype(jnp.float32),
        lax.psum_scatter(
            grad_outb.astype(jnp.bfloat16), "fsdp", scatter_dimension=0, tiled=True
        ).astype(jnp.float32),
        lax.psum_scatter(
            grad_gain_second.astype(jnp.bfloat16), "fsdp", scatter_dimension=0, tiled=True
        ).astype(jnp.float32),
        lax.psum_scatter(
            grad_bias_second.astype(jnp.bfloat16), "fsdp", scatter_dimension=0, tiled=True
        ).astype(jnp.float32),
        lax.psum_scatter(
            grad_up.astype(jnp.bfloat16), "fsdp", scatter_dimension=0, tiled=True
        ).astype(jnp.float32),
        lax.psum_scatter(
            grad_upb.astype(jnp.bfloat16), "fsdp", scatter_dimension=0, tiled=True
        ).astype(jnp.float32),
        lax.psum_scatter(
            grad_down.astype(jnp.bfloat16), "fsdp", scatter_dimension=1, tiled=True
        ).astype(jnp.float32),
        lax.psum_scatter(
            grad_downb.astype(jnp.bfloat16), "fsdp", scatter_dimension=0, tiled=True
        ).astype(jnp.float32),
    )
    (
        final_gone,
        final_bone,
        final_qkv,
        final_qvb,
        final_outw,
        final_outb,
        final_gtwo,
        final_btwo,
        final_up,
        final_upb,
        final_down,
        final_downb,
    ) = (
        lax.psum(part_gone.astype(jnp.bfloat16), "seq").astype(jnp.float32),
        lax.psum(part_bone.astype(jnp.bfloat16), "seq").astype(jnp.float32),
        lax.psum(part_qkv.astype(jnp.bfloat16), "seq").astype(jnp.float32),
        lax.psum(part_qvb.astype(jnp.bfloat16), "seq").astype(jnp.float32),
        lax.psum(part_outw.astype(jnp.bfloat16), "seq").astype(jnp.float32),
        lax.psum(part_outb.astype(jnp.bfloat16), "seq").astype(jnp.float32),
        lax.psum(part_gtwo.astype(jnp.bfloat16), "seq").astype(jnp.float32),
        lax.psum(part_btwo.astype(jnp.bfloat16), "seq").astype(jnp.float32),
        lax.psum(part_up.astype(jnp.bfloat16), "seq").astype(jnp.float32),
        lax.psum(part_upb.astype(jnp.bfloat16), "seq").astype(jnp.float32),
        lax.psum(part_down.astype(jnp.bfloat16), "seq").astype(jnp.float32),
        lax.psum(part_downb.astype(jnp.bfloat16), "seq").astype(jnp.float32),
    )
    return (
        layer_out,
        grad_images,
        final_gone,
        final_bone,
        final_qkv,
        final_qvb,
        final_outw,
        final_outb,
        final_gtwo,
        final_btwo,
        final_up,
        final_upb,
        final_down,
        final_downb,
    )


def solution(mesh):
    placed = (
        P("fsdp", "seq", None),
        P("fsdp"),
        P("fsdp"),
        P("fsdp"),
        P("fsdp", None),
        P(None, "fsdp"),
        P("fsdp", None),
        P("fsdp"),
        P("fsdp"),
        P("fsdp"),
        P("fsdp", None),
        P("fsdp"),
        P(None, "fsdp"),
        P("fsdp"),
        P("fsdp", "seq", None),
    )
    return jax.shard_map(
        on_device,
        mesh=mesh,
        in_specs=placed,
        out_specs=(
            P("fsdp", "seq", None),
            P("fsdp", "seq", None),
            P("fsdp"),
            P("fsdp"),
            P("fsdp", None),
            P(None, "fsdp"),
            P("fsdp", None),
            P("fsdp"),
            P("fsdp"),
            P("fsdp"),
            P("fsdp", None),
            P("fsdp"),
            P(None, "fsdp"),
            P("fsdp"),
        ),
        check_vma=False,
    )
```

profile of v0, /device:TPU:0, one launch (start us, length us, event | category | flops | bytes accessed | tf_op | source)
XLA Modules:
  0.0 1667.9 jit_solution(1936642603031009704)
XLA Ops:
  13.0 18.5 %all-reduce.17 = (bf16[1152]{0:T(1024)(128)(2,1)S(1)}, bf16[1152]{0:T(1024)(128)(2,1)S(1)}, bf16[1152]{0:T(1024)(128)(2,1)S(1)}, bf16[1152]{0:T(1024)(128)(2,1)S...) all-reduce(bf16[1152]{0:T(1024)(128)(2,1)S(1)} %dynamic-update-slic, ...), channel_id=1, replica_groups=mesh['fsdp'=4,'seq'=8] {'fsdp'}, use_global_device_ids=true, to_apply=%add.1 | all-reduce | flops 10064 | bytes 40256
  33.3 7.5 all-gather
  41.1 55.8 %all-gather.6.cloned.1.call-done = bf16[1152,3456]{1,0:T(8,128)(2,1)} async-done(((bf16[288,3456]{1,0:T(8,128)(2,1)}), bf16[1152,3456]{1,0:T(8,128)(2,1)}) %all-gather.6.cloned.1.call-update) | async-done | bytes 7962640 | tf_op jit(solution)/shard_map/all_gather | solution.py:113
  96.9 11.5 copy.97
  108.5 12.5 convolution_bitcast_fusion.3
  123.5 4.8 copy.99
  128.3 5.0 all-to-all-start
  133.9 155.1 %all-to-all-done = bf16[3,16,8,72,128]{4,3,0,2,1:T(8,128)(2,1)} async-done(((bf16[3,16,8,72,128]{4,3,0,2,1:T(8,128)(2,1)}), bf16[3,16,8,72,128]{4,3,0,2,1:T(8,128)(2,1)}, u32[]{:S(2)}, u32[]{:S(2)}) %all-to-all-start) | async-done | bytes 7077920 | tf_op jit(solution)/shard_map/all_to_all | solution.py:131
  289.0 7.7 fusion.114
  299.6 5.0 reshape_squeeze.10
  304.6 4.6 copy.102
  309.2 4.9 reshape_squeeze.11
  314.1 4.6 copy.100
  318.7 4.9 reshape_squeeze.9
  325.3 180.0 %while.26 = (s32[]{:T(128)}, bf16[16,72,1024]{2,1,0:T(8,128)(2,1)}, f32[16,1024]{1,0:T(8,128)}, bf16[16,72,1024]{2,1,0:T(8,128)(2,1)}, s32[16]{0:T(128)S(1)}, /*...) while((s32[]{:T(128)}, bf16[16,72,1024]{2,1,0:T(8,128)(2,1)}, ...), condition=%wide.region_5.6_spmd, body=%wide.region_2.5_spmd.sunk | while | flops 311500800 | bytes 29997196 | solution.py:138
  505.4 6.3 copy.103
  511.7 4.5 all-to-all-start.1
  516.7 93.5 %all-to-all-done.1 = bf16[2,8,72,1024]{2,1,0,3:T(8,128)(2,1)} async-done(((bf16[2,8,72,1024]{2,1,0,3:T(8,128)(2,1)}), bf16[2,8,72,1024]{2,1,0,3:T(8,128)(2,1)}, u32[]{:S(2)}, u32[]{:S(2)}) %all-to-all-start.1) | async-done | bytes 2359328 | tf_op jit(solution)/shard_map/all_to_all | solution.py:141
  610.2 6.3 copy.105
  616.5 6.5 fusion.116
  625.9 24.8 %multiply_convert_fusion.1 = (bf16[8,128,4304]{1,2,0:T(8,128)(2,1)}, f32[8,128,4304]{1,2,0:T(8,128)}) fusion(f32[4304]{0:T(1024)S(1)} %convert_element_type.186, bf16[1152,4304]{1,0:T(8,128)(2,1)} %all-gather.10.cloned.1.call-done, f32[8,128,1152]{2,1,0:T(8,128)} %copy-done.5, f32[1152]{0:T(1024)S(1)} %convert_element_type.184, ...), kind=kOutput, calls=%fused_computation.72 | convolution fusion | flops 10204381184 | bytes 41113408 | tf_op jit(solution)/shard_map/itd,df->itf/dot_general | solution.py:166
  650.7 32.5 %fusion.117 = (bf16[4304]{0:T(1024)(128)(2,1)}, bf16[8,128,4304]{1,2,0:T(8,128)(2,1)}) fusion(f32[8,128,4304]{1,2,0:T(8,128)} %get-tuple-element.199, f32[4304]{0:T(1024)S(1)} %convert_element_type.186, bf16[8,128,1152]{2,1,0:T(8,128)(2,1)} %param.34, bf16[4304,1152]{0,1:T(8,128)(2,1)} %all-gather.12.cloned.1.call-done), kind=kOutput, calls=%fused_computation.155 | convolution fusion | flops 10251366400 | bytes 38745312 | tf_op jit(solution)/shard_map/itd,fd->itf/dot_general | solution.py:187
  683.2 20.6 %multiply_reduce_fusion.1 = (bf16[1152]{0:T(1024)(128)(2,1)}, f32[8,128]{1,0:T(8,128)S(1)}, bf16[1152]{0:T(1024)(128)(2,1)}, f32[8,128,1152]{2,1,0:T(8,128)}) fusion(f32[8,128,1152]{2,1,0:T(8,128)S(1)} %bitcast.254, f32[8,128]{1,0:T(8,128)S(1)} %fusion.109, f32[8,128]{1,0:T(8,128)S(1)} %broadcast_multiply_fusion, f32[1152]{0:T(1024)S(1)} %convert_element_type.183, ...), kind=kOutput, calls=%fused_computation.117 | convolution fusion | flops 10163844096 | bytes 28189696 | tf_op jit(solution)/shard_map/itf,df->itd/dot_general | solution.py:192
  710.9 4.4 fusion.71
  715.4 19.1 %fusion.54 = bf16[1152,4304]{1,0:T(8,128)(2,1)} fusion(bf16[8,128,4304]{1,2,0:T(8,128)(2,1)} %get-tuple-element.203, f32[8,128,1152]{2,1,0:T(8,128)} %copy-done.5, f32[1152]{0:T(1024)S(1)} %convert_element_type.184, f32[1152]{0:T(1024)S(1)} %convert_element_type.183, f32[8,128]{1,0:T(8,128)S(1)} %fusion.109, f32[8,128]{1,0:T(8,128)S(1)} %broadcast_multiply_fusion), kind=kOutput, calls=%fused_computation.63 | convolution fusion | flops 10165266432 | bytes 23467008 | tf_op jit(solution)/shard_map/itd,itf->df/dot_general | solution.py:190
  736.3 4.8 convert_bitcast_fusion
  747.3 16.5 fusion.55
  764.1 37.8 %all-to-all-done.2 = bf16[16,8,72,128]{3,2,1,0:T(8,128)(2,1)} async-done(((bf16[16,8,72,128]{3,2,1,0:T(8,128)(2,1)}), bf16[16,8,72,128]{3,2,1,0:T(8,128)(2,1)}, u32[]{:S(2)}, u32[]{:S(2)}) %all-to-all-start.2) | async-done | bytes 2359328 | tf_op jit(solution)/shard_map/all_to_all | solution.py:206
  811.2 220.9 %while.27 = (s32[]{:T(128)}, bf16[16,72,1024]{2,1,0:T(8,128)(2,1)S(1)}, bf16[16,72,1024]{2,1,0:T(8,128)(2,1)}, bf16[16,72,1024]{2,1,0:T(8,128)(2,1)}, bf16[16,72...) while((s32[]{:T(128)}, ...), condition=%wide.region_12.13_spmd, body=%wide.region_10.12_spmd.sunk | while | flops 767778816 | bytes 32969856 | solution.py:208
  1032.1 4.9 copy.108
  1037.0 6.4 copy.109
  1043.4 6.3 copy.110
  1049.7 6.9 pad_maximum_fusion
  1056.7 277.4 %all_to_all.66 = bf16[3,2,8,72,1024]{3,2,1,0,4:T(8,128)(2,1)} all-to-all(bf16[3,2,8,72,1024]{3,2,1,0,4:T(8,128)(2,1)S(1)} %pad_maximum_fusion), channel_id=1, replica_groups=mesh['fsdp'=4,'seq'=8] {'seq'}, dimensions={4} | all-to-all | bytes 14155776 | tf_op jit(solution)/shard_map/all_to_all | solution.py:213
  1334.1 15.4 copy.114
  1349.5 13.9 fusion.63
  1363.4 11.6 copy.115
  1376.8 13.2 copy.133
  1390.1 4.5 convert_reduce_fusion
  1405.6 5.8 fusion.98
  1411.4 8.9 fusion.110
  1424.5 17.1 %all-reduce.16 = (bf16[1152]{0:T(1024)(128)(2,1)S(1)}, bf16[1152]{0:T(1024)(128)(2,1)S(1)}, bf16[1152]{0:T(1024)(128)(2,1)S(1)}, bf16[1152]{0:T(1024)(128)(2,1)S...) all-reduce(bf16[1152]{0:T(1024)(128)(2,1)S(1)} %dynamic-update-slic, ...), channel_id=1, replica_groups=mesh['fsdp'=4,'seq'=8] {'fsdp'}, use_global_device_ids=true, to_apply=%add.6 | all-reduce | flops 12368 | bytes 49472
  1442.2 15.3 reduce-scatter.8.cloned.1.call-done
  1457.5 6.5 add_convert_fusion
  1464.1 19.0 %fusion.94 = bf16[8,128,1152]{2,1,0:T(8,128)(2,1)} fusion(f32[8,128,1152]{2,1,0:T(8,128)} %copy-done.5, bf16[8,128,4304]{1,2,0:T(8,128)(2,1)} %get-tuple-element.198, bf16[4304,1152]{0,1:T(8,128)(2,1)} %all-gather.12.cloned.1.call-done, f32[1152]{0:T(1024)S(1)} %convert_element_type.188), kind=kOutput, calls=%fused_computation.123 | convolution fusion | flops 10157948928 | bytes 25813504 | tf_op jit(solution)/shard_map/itf,fd->itd/dot_general | solution.py:173
  1486.2 29.3 %all-reduce.14 = (bf16[288]{0:T(512)(128)(2,1)S(1)}, bf16[288]{0:T(512)(128)(2,1)S(1)}, bf16[2,288]{1,0:T(2,128)(2,1)S(1)}, bf16[288]{0:T(512)(128)(2,1)S(1)}, b...) all-reduce(bf16[288]{0:T(512)(128)(2,1)S(1)} %dynamic-slice.8, ...), channel_id=1, replica_groups=mesh['fsdp'=4,'seq'=8] {'seq'}, use_global_device_ids=true, to_apply=%region_17.18 | all-reduce | flops 3380 | bytes 13520 | tf_op jit(solution)/shard_map/psum | solution.py:302
  1520.2 130.0 %all-reduce.20.cloned.1.call-done = (bf16[288,3456]{1,0:T(8,128)(2,1)}, bf16[288,1152]{1,0:T(8,128)(2,1)}, bf16[288,4304]{1,0:T(8,128)(2,1)}, bf16[4304,288]{0,1:T(8,128)(2,1)}) async-done(((bf16[288,3456]{1,0:T(8,128)(2,1)}, bf16[288,1152]{1,0:T(8,128)(2,1)}, bf16[288,4304]{1,0:T(8,128)(2,1)}, bf16[4304,288]{0,1:T(8,128)(2,1)}), (bf16[288,3456]{1,0:T(8,128)(2,1)}, bf16[288,1152]{1,0:T(8,128)(2,1)}, ...) | async-done | bytes 7612432 | tf_op jit(solution)/shard_map/psum | solution.py:304
  1650.2 4.5 convert_element_type.213
  (502 shorter events, 471.8 us)
Async XLA Ops:
  7.2 4.2 copy-start.35
  7.2 4.5 copy-start.36
  7.2 4.7 copy-start.37
  7.2 5.0 copy-start.38
  7.2 5.2 copy-start.39
  7.2 5.5 copy-start.32
  7.3 24.2 %copy-start.2 = (bf16[8,128,1152]{2,1,0:T(8,128)(2,1)S(1)}, bf16[8,128,1152]{2,1,0:T(8,128)(2,1)}, u32[]{:S(2)}) copy-start(bf16[8,128,1152]{2,1,0:T(8,128)(2,1)} %param.20) | copy-start | bytes 7077892
  7.3 26.0 %copy-start.34 = (bf16[2,288]{1,0:T(2,128)(2,1)S(1)}, bf16[2,288]{1,0:T(2,128)(2,1)}, u32[]{:S(2)}) copy-start(bf16[2,288]{1,0:T(2,128)(2,1)} %param.25) | copy-start | bytes 3460
  7.3 89.6 %all-gather.6.cloned.1.call-start = ((), (), s32[]{:S(2)}) async-start(), calls=%async_computation.9 | async-start | bytes 9953280 | tf_op jit(solution)/shard_map/all_gather | solution.py:113
  8.0 608.5 %all-gather.8.cloned.1.call-start = ((), (), s32[]{:S(2)}) async-start(), calls=%async_computation.10 | async-start | bytes 3317760 | tf_op jit(solution)/shard_map/all_gather | solution.py:115
  8.8 617.1 %all-gather.10.cloned.1.call-start = ((), (), s32[]{:S(2)}) async-start(), calls=%async_computation.11 | async-start | bytes 12533760 | tf_op jit(solution)/shard_map/all_gather | solution.py:157
  31.5 77.0 %copy-start.15 = (f32[1152]{0:T(1024)}, f32[1152]{0:T(1024)S(1)}, u32[]{:S(2)}) copy-start(f32[1152]{0:T(1024)S(1)} %convert_element_type.178) | copy-start | bytes 13828
  31.5 77.0 %copy-start.28 = (f32[1152]{0:T(1024)}, f32[1152]{0:T(1024)S(1)}, u32[]{:S(2)}) copy-start(f32[1152]{0:T(1024)S(1)} %convert_element_type.179) | copy-start | bytes 13828
  31.9 76.6 %copy-start.17 = (f32[8,128]{1,0:T(8,128)}, f32[8,128]{1,0:T(8,128)S(1)}, u32[]{:S(2)}) copy-start(f32[8,128]{1,0:T(8,128)S(1)} %broadcast_multiply_fusion.1) | copy-start | bytes 12292
  32.7 75.8 %copy-start.21 = (f32[8,128]{1,0:T(8,128)}, f32[8,128]{1,0:T(8,128)S(1)}, u32[]{:S(2)}) copy-start(f32[8,128]{1,0:T(8,128)S(1)} %fusion.108) | copy-start | bytes 12292
  128.3 5.6 copy-start.41
  128.3 160.7 %all-to-all-start = ((bf16[3,16,8,72,128]{4,3,0,2,1:T(8,128)(2,1)}), bf16[3,16,8,72,128]{4,3,0,2,1:T(8,128)(2,1)}, u32[]{:S(2)}, u32[]{:S(2)}) async-start(bf16[3,16,8,72,128]{4,3,0,2,1:T(8,128)(2,1)} %copy.99), calls=%async_computation | async-start | bytes 14155776 | tf_op jit(solution)/shard_map/all_to_all | solution.py:131
  133.2 517.4 %all-gather.12.cloned.1.call-start = ((), (), s32[]{:S(2)}) async-start(), calls=%async_computation.12 | async-start | bytes 12533760 | tf_op jit(solution)/shard_map/all_gather | solution.py:159
  505.4 6.3 copy-start.42
  511.7 98.5 %all-to-all-start.1 = ((bf16[2,8,72,1024]{2,1,0,3:T(8,128)(2,1)}), bf16[2,8,72,1024]{2,1,0,3:T(8,128)(2,1)}, u32[]{:S(2)}, u32[]{:S(2)}) async-start(bf16[2,8,72,1024]{2,1,0,3:T(8,128)(2,1)} %bitcast.255), calls=%async_computation.1 | async-start | bytes 8388608 | tf_op jit(solution)/shard_map/all_to_all | solution.py:141
  516.2 926.0 %reduce-scatter.10.cloned.1.call-start = ((), (), s32[]{:S(2)}) async-start(), calls=%async_computation.14 | async-start | bytes 3317760 | tf_op jit(solution)/shard_map/reduce_scatter | solution.py:263
  625.9 57.3 %slice-start = ((s8[4718592]{0:T(1024)(128)(4,1)}), s8[524288]{0:T(1024)(128)(4,1)S(1)}, s32[]{:S(2)}) async-start(s8[4718592]{0:T(1024)(128)(4,1)} %bitcast.253), calls=%async_computation.19 | async-start | bytes 1048576
  650.7 32.5 %slice-start.1 = ((s8[4718592]{0:T(1024)(128)(4,1)}), s8[4194304]{0:T(1024)(128)(4,1)S(1)}, s32[]{:S(2)}) async-start(s8[4718592]{0:T(1024)(128)(4,1)} %bitcast.253), calls=%async_computation.20 | async-start | bytes 8388608
  707.1 3.8 copy-start.9
  715.4 726.9 %reduce-scatter.12.cloned.1.call-start = ((), (), s32[]{:S(2)}) async-start(), calls=%async_computation.15 | async-start | bytes 12533760 | tf_op jit(solution)/shard_map/reduce_scatter | solution.py:275
  741.1 6.2 copy-start.8
  742.9 59.0 %all-to-all-start.2 = ((bf16[16,8,72,128]{3,2,1,0:T(8,128)(2,1)}), bf16[16,8,72,128]{3,2,1,0:T(8,128)(2,1)}, u32[]{:S(2)}, u32[]{:S(2)}) async-start(bf16[16,8,72,128]{3,2,1,0:T(8,128)(2,1)} %copy.106), calls=%async_computation.2 | async-start | bytes 4718592 | tf_op jit(solution)/shard_map/all_to_all | solution.py:206
  747.2 695.0 %reduce-scatter.14.cloned.1.call-start = ((), (), s32[]{:S(2)}) async-start(), calls=%async_computation.16 | async-start | bytes 12533760 | tf_op jit(solution)/shard_map/reduce_scatter | solution.py:281
  763.8 693.7 %reduce-scatter.8.cloned.1.call-start = ((), (), s32[]{:S(2)}) async-start(), calls=%async_computation.13 | async-start | bytes 9953280 | tf_op jit(solution)/shard_map/reduce_scatter | solution.py:257
  1334.0 15.4 copy-start.3
  1334.0 15.4 copy-start.16
  1334.0 15.4 copy-start.18
  1334.0 15.4 copy-start.22
  1334.0 15.4 copy-start.29
  1334.1 15.4 copy-start.44
  1375.0 110.2 %reduce-scatter.16.cloned.1.call-start = ((), (), s32[]{:S(2)}) async-start(), calls=%async_computation.17 | async-start | bytes 368640
  1390.1 5.6 copy-start.1
  1404.5 6.8 slice-start.2
  1405.6 5.8 slice-start.3
  1411.4 8.9 copy-start.24
  1420.3 4.1 copy-start.25
  1420.3 4.1 copy-start.26
  1420.3 4.1 copy-start.27
  1420.3 4.2 copy-start.30
  1420.3 4.2 copy-start.31
  1420.4 229.8 %all-reduce.20.cloned.1.call-start = ((), (), s32[]{:S(2)}) async-start(), calls=%async_computation.18 | async-start | bytes 15335424 | tf_op jit(solution)/shard_map/psum | solution.py:304
  1424.4 33.1 %copy-start.20 = (f32[8,128]{1,0:T(8,128)S(1)}, f32[8,128]{1,0:T(8,128)}, u32[]{:S(2)}) copy-start(f32[8,128]{1,0:T(8,128)} %copy-done.19) | copy-start | bytes 12292
  1650.2 4.5 copy-start.11
  (29 other events, 62.1 us)
Sparse Core Ops, SparseCore 0:
  9.9 86.9 all-gather.5
  98.8 39.7 all-gather.7
  140.4 101.0 all-gather.9
  243.3 101.0 all-gather.11
  715.5 38.3 reduce-scatter.9
  756.9 99.6 reduce-scatter.11
  859.8 99.6 reduce-scatter.13
  1375.1 82.3 reduce-scatter.7
  1460.8 24.3 reduce-scatter.15
  1487.7 162.3 all-reduce.19
where the time goes:
time: 1680 us; the launch traced here: 1670 us
  waiting for transfers between devices  492 us (29%)
  matrix products  447 us (27%)
  blocking collectives  350 us (21%)
  local copies, waits for them, and re-layouts  242 us (14%)
  other arithmetic  102 us (6%)
  between operations  18 us (1%)
    all_to_all x1, blocking collectives, on_device(): lax.all_to_all(for_sending(grad_stack), 'seq', split_axis=4, concat_axis=...  277 us
    all_to_all x1, waiting for transfers between devices, on_device(): lax.all_to_all(stacked, 'seq', split_axis=1, concat_axis=4, tiled=True)  155 us
    psum x1, waiting for transfers between devices, on_device(): lax.psum(part_qkv.astype(jnp.bfloat16), 'seq').astype(jnp.float32)  130 us
    all_to_all x1, waiting for transfers between devices, on_device(): lax.all_to_all(for_sending(mixed_items.reshape(local_heads, image_count,...  93.5 us
    dot_general x16, matrix products, attend_item(): jnp.einsum('qk,dk->dq', softmax_low, values, preferred_element_type=jnp.f...  64.5 us
    all_gather x1, waiting for transfers between devices, on_device(): lax.all_gather(w_qkv, 'fsdp', axis=0, tiled=True)  55.8 us
    dot_general x16, matrix products, attend_back(): jnp.einsum('qk,dq->dk', softmax_out.astype(jnp.bfloat16), grad_rows, pref...  42.4 us
    all_to_all x1, waiting for transfers between devices, on_device(): lax.all_to_all(grad_mixed, 'seq', split_axis=0, concat_axis=3, tiled=True)  37.8 us
  transfers between devices with their start and end apart: 13, of which 7 were waited for; matrix products, arithmetic and copies ran while one was open for 41% of the time, Pallas kernels for 0%

commit v1 on v0

--- a/solution.py
+++ b/solution.py
@@ -285,6 +285,11 @@
             grad_downb.astype(jnp.bfloat16), "fsdp", scatter_dimension=0, tiled=True
         ).astype(jnp.float32),
     )
+
+    def do_values(content, bus_axis):
+        local_now = lax.all_gather(content, bus_axis)
+        return jnp.sum(local_now, 0)
+
     (
         final_gone,
         final_bone,
@@ -301,7 +306,7 @@
     ) = (
         lax.psum(part_gone.astype(jnp.bfloat16), "seq").astype(jnp.float32),
         lax.psum(part_bone.astype(jnp.bfloat16), "seq").astype(jnp.float32),
-        lax.psum(part_qkv.astype(jnp.bfloat16), "seq").astype(jnp.float32),
+        do_values(part_qkv.astype(jnp.bfloat16), "seq").astype(jnp.float32),
         lax.psum(part_qvb.astype(jnp.bfloat16), "seq").astype(jnp.float32),
         lax.psum(part_outw.astype(jnp.bfloat16), "seq").astype(jnp.float32),
         lax.psum(part_outb.astype(jnp.bfloat16), "seq").astype(jnp.float32),

time: 1680 us -> 1790 us (1.065)
  waiting for transfers between devices: 492 us -> 597 us
    all_gather x0 -> x1, waiting for transfers between devices: none -> 137 us  [do_values(): local_now = lax.all_gather(content, bus_axis)]
    psum x1, waiting for transfers between devices: 130 us -> 53.2 us  [on_device(): lax.psum(part_outw.astype(jnp.bfloat16), 'seq').astype(jnp.float32)]
    reduce_scatter x1, waiting for transfers between devices: 15.3 us -> 60.8 us  [on_device(): lax.psum_scatter(grad_qkv.astype(jnp.bfloat16), 'fsdp', scatter_dimension...]
  transfers between devices with their start and end apart: 13 -> 14, of which waited for: 7 -> 7; matrix products, arithmetic and copies ran while one was open for 41% -> 38% of each run, Pallas kernels for 0% -> 0%
where the time goes in v1:
time: 1790 us; the launch traced here: 1780 us
  waiting for transfers between devices  597 us (33%)
  matrix products  447 us (25%)
  blocking collectives  348 us (19%)
  local copies, waits for them, and re-layouts  241 us (13%)
  other arithmetic  110 us (6%)
    all_to_all x1, blocking collectives, on_device(): lax.all_to_all(for_sending(grad_stack), 'seq', split_axis=4, concat_axis=...  278 us
    all_to_all x1, waiting for transfers between devices, on_device(): lax.all_to_all(stacked, 'seq', split_axis=1, concat_axis=4, tiled=True)  155 us
    all_gather x1, waiting for transfers between devices, do_values(): local_now = lax.all_gather(content, bus_axis)  137 us
    all_to_all x1, waiting for transfers between devices, on_device(): lax.all_to_all(for_sending(mixed_items.reshape(local_heads, image_count,...  93.7 us
    dot_general x16, matrix products, attend_item(): jnp.einsum('qk,dk->dq', softmax_low, values, preferred_element_type=jnp.f...  64.5 us
    reduce_scatter x1, waiting for transfers between devices, on_device(): lax.psum_scatter(grad_qkv.astype(jnp.bfloat16), 'fsdp', scatter_dimension...  60.8 us
    all_gather x1, waiting for transfers between devices, on_device(): lax.all_gather(w_qkv, 'fsdp', axis=0, tiled=True)  55.8 us
    psum x1, waiting for transfers between devices, on_device(): lax.psum(part_outw.astype(jnp.bfloat16), 'seq').astype(jnp.float32)  53.2 us
  transfers between devices with their start and end apart: 14, of which 7 were waited for; matrix products, arithmetic and copies ran while one was open for 38% of the time, Pallas kernels for 0%

profile of v1, /device:TPU:0, one launch (start us, length us, event | category | flops | bytes accessed | tf_op | source)
XLA Modules:
  0.0 1776.6 jit_solution(1051532174281180062)
XLA Ops:
  13.0 18.5 %all-reduce.17 = (bf16[1152]{0:T(1024)(128)(2,1)S(1)}, bf16[1152]{0:T(1024)(128)(2,1)S(1)}, bf16[1152]{0:T(1024)(128)(2,1)S(1)}, bf16[1152]{0:T(1024)(128)(2,1)S...) all-reduce(bf16[1152]{0:T(1024)(128)(2,1)S(1)} %dynamic-update-slic, ...), channel_id=1, replica_groups=mesh['fsdp'=4,'seq'=8] {'fsdp'}, use_global_device_ids=true, to_apply=%add.1 | all-reduce | flops 10064 | bytes 40256
  33.3 7.6 all-gather.1
  41.2 55.8 %all-gather.8.cloned.1.call-done = bf16[1152,3456]{1,0:T(8,128)(2,1)} async-done(((bf16[288,3456]{1,0:T(8,128)(2,1)}), bf16[1152,3456]{1,0:T(8,128)(2,1)}) %all-gather.8.cloned.1.call-update) | async-done | bytes 7962640 | tf_op jit(solution)/shard_map/all_gather | solution.py:113
  96.9 11.6 copy.96
  108.5 12.5 convolution_bitcast_fusion.3
  123.5 4.7 copy.98
  128.3 5.0 all-to-all-start
  133.9 155.1 %all-to-all-done = bf16[3,16,8,72,128]{4,3,0,2,1:T(8,128)(2,1)} async-done(((bf16[3,16,8,72,128]{4,3,0,2,1:T(8,128)(2,1)}), bf16[3,16,8,72,128]{4,3,0,2,1:T(8,128)(2,1)}, u32[]{:S(2)}, u32[]{:S(2)}) %all-to-all-start) | async-done | bytes 7077920 | tf_op jit(solution)/shard_map/all_to_all | solution.py:131
  289.0 7.7 fusion.114
  299.6 4.9 reshape_squeeze.10
  304.5 4.6 copy.101
  309.1 4.9 reshape_squeeze.11
  314.1 4.6 copy.99
  318.7 4.9 reshape_squeeze.9
  325.3 180.0 %while.26 = (s32[]{:T(128)}, bf16[16,72,1024]{2,1,0:T(8,128)(2,1)}, f32[16,1024]{1,0:T(8,128)}, bf16[16,72,1024]{2,1,0:T(8,128)(2,1)}, s32[16]{0:T(128)S(1)}, /*...) while((s32[]{:T(128)}, bf16[16,72,1024]{2,1,0:T(8,128)(2,1)}, ...), condition=%wide.region_5.6_spmd, body=%wide.region_2.5_spmd.sunk | while | flops 311500800 | bytes 29997196 | solution.py:138
  505.3 6.3 copy.102
  511.6 4.6 all-to-all-start.1
  516.5 93.7 %all-to-all-done.1 = bf16[2,8,72,1024]{2,1,0,3:T(8,128)(2,1)} async-done(((bf16[2,8,72,1024]{2,1,0,3:T(8,128)(2,1)}), bf16[2,8,72,1024]{2,1,0,3:T(8,128)(2,1)}, u32[]{:S(2)}, u32[]{:S(2)}) %all-to-all-start.1) | async-done | bytes 2359328 | tf_op jit(solution)/shard_map/all_to_all | solution.py:141
  610.2 6.3 copy.104
  616.5 6.5 fusion.116
  625.9 24.8 %multiply_convert_fusion.1 = (bf16[8,128,4304]{1,2,0:T(8,128)(2,1)}, f32[8,128,4304]{1,2,0:T(8,128)}) fusion(f32[4304]{0:T(1024)S(1)} %convert_element_type.188, bf16[1152,4304]{1,0:T(8,128)(2,1)} %all-gather.12.cloned.1.call-done, f32[8,128,1152]{2,1,0:T(8,128)} %copy-done.4, f32[1152]{0:T(1024)S(1)} %convert_element_type.186, ...), kind=kOutput, calls=%fused_computation.72 | convolution fusion | flops 10204381184 | bytes 41113408 | tf_op jit(solution)/shard_map/itd,df->itf/dot_general | solution.py:166
  650.7 32.5 %fusion.117 = (bf16[4304]{0:T(1024)(128)(2,1)}, bf16[8,128,4304]{1,2,0:T(8,128)(2,1)}) fusion(f32[8,128,4304]{1,2,0:T(8,128)} %get-tuple-element.198, f32[4304]{0:T(1024)S(1)} %convert_element_type.188, bf16[8,128,1152]{2,1,0:T(8,128)(2,1)} %param.34, bf16[4304,1152]{0,1:T(8,128)(2,1)} %all-gather.14.cloned.1.call-done), kind=kOutput, calls=%fused_computation.155 | convolution fusion | flops 10251366400 | bytes 38745312 | tf_op jit(solution)/shard_map/itd,fd->itf/dot_general | solution.py:187
  683.2 20.8 %multiply_reduce_fusion.1 = (bf16[1152]{0:T(1024)(128)(2,1)}, f32[8,128]{1,0:T(8,128)S(1)}, bf16[1152]{0:T(1024)(128)(2,1)}, f32[8,128,1152]{2,1,0:T(8,128)}) fusion(f32[8,128,1152]{2,1,0:T(8,128)S(1)} %bitcast.255, f32[8,128]{1,0:T(8,128)S(1)} %fusion.109, f32[8,128]{1,0:T(8,128)S(1)} %broadcast_multiply_fusion, f32[1152]{0:T(1024)S(1)} %convert_element_type.185, ...), kind=kOutput, calls=%fused_computation.117 | convolution fusion | flops 10163844096 | bytes 28189696 | tf_op jit(solution)/shard_map/itf,df->itd/dot_general | solution.py:192
  715.7 18.9 %fusion.54 = bf16[1152,4304]{1,0:T(8,128)(2,1)} fusion(bf16[8,128,4304]{1,2,0:T(8,128)(2,1)} %get-tuple-element.202, f32[8,128,1152]{2,1,0:T(8,128)} %copy-done.4, f32[1152]{0:T(1024)S(1)} %convert_element_type.186, f32[1152]{0:T(1024)S(1)} %convert_element_type.185, f32[8,128]{1,0:T(8,128)S(1)} %fusion.109, f32[8,128]{1,0:T(8,128)S(1)} %broadcast_multiply_fusion), kind=kOutput, calls=%fused_computation.63 | convolution fusion | flops 10165266432 | bytes 23467008 | tf_op jit(solution)/shard_map/itd,itf->df/dot_general | solution.py:190
  736.4 4.8 convert_bitcast_fusion
  747.4 16.3 fusion.55
  764.0 38.0 %all-to-all-done.2 = bf16[16,8,72,128]{3,2,1,0:T(8,128)(2,1)} async-done(((bf16[16,8,72,128]{3,2,1,0:T(8,128)(2,1)}), bf16[16,8,72,128]{3,2,1,0:T(8,128)(2,1)}, u32[]{:S(2)}, u32[]{:S(2)}) %all-to-all-start.2) | async-done | bytes 2359328 | tf_op jit(solution)/shard_map/all_to_all | solution.py:206
  811.4 220.9 %while.27 = (s32[]{:T(128)}, bf16[16,72,1024]{2,1,0:T(8,128)(2,1)S(1)}, bf16[16,72,1024]{2,1,0:T(8,128)(2,1)}, bf16[16,72,1024]{2,1,0:T(8,128)(2,1)}, bf16[16,72...) while((s32[]{:T(128)}, ...), condition=%wide.region_12.13_spmd, body=%wide.region_10.12_spmd.sunk | while | flops 767778816 | bytes 32969856 | solution.py:208
  1032.2 4.9 copy.107
  1037.1 6.4 copy.108
  1043.5 6.3 copy.109
  1049.8 6.9 pad_maximum_fusion
  1056.8 278.2 %all_to_all.66 = bf16[3,2,8,72,1024]{3,2,1,0,4:T(8,128)(2,1)} all-to-all(bf16[3,2,8,72,1024]{3,2,1,0,4:T(8,128)(2,1)S(1)} %pad_maximum_fusion), channel_id=1, replica_groups=mesh['fsdp'=4,'seq'=8] {'seq'}, dimensions={4} | all-to-all | bytes 14155776 | tf_op jit(solution)/shard_map/all_to_all | solution.py:213
  1335.0 15.3 copy.113
  1350.4 13.9 fusion.63
  1364.3 11.5 copy.114
  1375.9 13.5 copy.132
  1396.3 60.8 %reduce-scatter.8.cloned.1.call-done = bf16[288,3456]{1,0:T(8,128)(2,1)} async-done(((bf16[1152,3456]{1,0:T(8,128)(2,1)}), bf16[288,3456]{1,0:T(8,128)(2,1)}) %reduce-scatter.8.cloned.1.call-update) | async-done | bytes 1990672 | tf_op jit(solution)/shard_map/reduce_scatter | solution.py:257
  1465.6 5.2 fusion.98
  1470.8 9.2 fusion.110
  1484.4 16.0 all-reduce.16
  1501.0 6.7 add_convert_fusion
  1507.7 19.1 %fusion.94 = bf16[8,128,1152]{2,1,0:T(8,128)(2,1)} fusion(f32[8,128,1152]{2,1,0:T(8,128)} %copy-done.4, bf16[8,128,4304]{1,2,0:T(8,128)(2,1)} %get-tuple-element.197, bf16[4304,1152]{0,1:T(8,128)(2,1)} %all-gather.14.cloned.1.call-done, f32[1152]{0:T(1024)S(1)} %convert_element_type.190), kind=kOutput, calls=%fused_computation.123 | convolution fusion | flops 10157948928 | bytes 25813504 | tf_op jit(solution)/shard_map/itf,fd->itd/dot_general | solution.py:173
  1527.7 27.2 %all-reduce.14 = (bf16[288]{0:T(512)(128)(2,1)S(1)}, bf16[288]{0:T(512)(128)(2,1)S(1)}, bf16[2,288]{1,0:T(2,128)(2,1)S(1)}, bf16[288]{0:T(512)(128)(2,1)S(1)}, b...) all-reduce(bf16[288]{0:T(512)(128)(2,1)S(1)} %dynamic-slice.8, ...), channel_id=1, replica_groups=mesh['fsdp'=4,'seq'=8] {'seq'}, use_global_device_ids=true, to_apply=%region_17.18 | all-reduce | flops 3380 | bytes 13520 | tf_op jit(solution)/shard_map/psum | solution.py:307
  1559.6 53.2 %all-reduce.20.cloned.1.call-done = (bf16[288,1152]{1,0:T(8,128)(2,1)}, bf16[288,4304]{1,0:T(8,128)(2,1)}, bf16[4304,288]{0,1:T(8,128)(2,1)}) async-done(((bf16[288,1152]{1,0:T(8,128)(2,1)}, bf16[288,4304]{1,0:T(8,128)(2,1)}, bf16[4304,288]{0,1:T(8,128)(2,1)}), (bf16[288,1152]{1,0:T(8,128)(2,1)}, bf16[288,4304]{1,0:T(8,128)(2,1)}, bf16[4304,288]{0,1:T(8,128)(2,1)})) %all-reduce.20.cloned.1.call-update) | async-done | bytes 5621776 | tf_op jit(solution)/shard_map/psum | solution.py:311
  1612.8 4.5 convert_element_type.215
  1621.0 137.5 %all-gather.16.cloned.1.call-done = bf16[2304,3456]{1,0:T(8,128)(2,1)} async-done(((bf16[288,3456]{1,0:T(8,128)(2,1)}), bf16[2304,3456]{1,0:T(8,128)(2,1)}) %all-gather.16.cloned.1.call-update) | async-done | bytes 15925264 | tf_op jit(solution)/shard_map/all_gather | solution.py:290
  1758.5 9.1 reduce_sum.225
  (502 shorter events, 476.7 us)
Async XLA Ops:
  7.2 4.2 copy-start.33
  7.2 4.5 copy-start.34
  7.2 4.7 copy-start.35
  7.2 5.0 copy-start.36
  7.2 5.2 copy-start.37
  7.2 5.5 copy-start.30
  7.3 24.2 %copy-start.1 = (bf16[8,128,1152]{2,1,0:T(8,128)(2,1)S(1)}, bf16[8,128,1152]{2,1,0:T(8,128)(2,1)}, u32[]{:S(2)}) copy-start(bf16[8,128,1152]{2,1,0:T(8,128)(2,1)} %param.20) | copy-start | bytes 7077892
  7.3 26.0 %copy-start.32 = (bf16[2,288]{1,0:T(2,128)(2,1)S(1)}, bf16[2,288]{1,0:T(2,128)(2,1)}, u32[]{:S(2)}) copy-start(bf16[2,288]{1,0:T(2,128)(2,1)} %param.25) | copy-start | bytes 3460
  7.3 89.6 %all-gather.8.cloned.1.call-start = ((), (), s32[]{:S(2)}) async-start(), calls=%async_computation.9 | async-start | bytes 9953280 | tf_op jit(solution)/shard_map/all_gather | solution.py:113
  8.0 608.5 %all-gather.10.cloned.1.call-start = ((), (), s32[]{:S(2)}) async-start(), calls=%async_computation.10 | async-start | bytes 3317760 | tf_op jit(solution)/shard_map/all_gather | solution.py:115
  8.8 617.1 %all-gather.12.cloned.1.call-start = ((), (), s32[]{:S(2)}) async-start(), calls=%async_computation.11 | async-start | bytes 12533760 | tf_op jit(solution)/shard_map/all_gather | solution.py:157
  31.5 77.0 %copy-start.13 = (f32[1152]{0:T(1024)}, f32[1152]{0:T(1024)S(1)}, u32[]{:S(2)}) copy-start(f32[1152]{0:T(1024)S(1)} %convert_element_type.180) | copy-start | bytes 13828
  31.5 77.0 %copy-start.26 = (f32[1152]{0:T(1024)}, f32[1152]{0:T(1024)S(1)}, u32[]{:S(2)}) copy-start(f32[1152]{0:T(1024)S(1)} %convert_element_type.181) | copy-start | bytes 13828
  31.9 76.6 %copy-start.15 = (f32[8,128]{1,0:T(8,128)}, f32[8,128]{1,0:T(8,128)S(1)}, u32[]{:S(2)}) copy-start(f32[8,128]{1,0:T(8,128)S(1)} %broadcast_multiply_fusion.1) | copy-start | bytes 12292
  32.7 75.8 %copy-start.19 = (f32[8,128]{1,0:T(8,128)}, f32[8,128]{1,0:T(8,128)S(1)}, u32[]{:S(2)}) copy-start(f32[8,128]{1,0:T(8,128)S(1)} %fusion.108) | copy-start | bytes 12292
  128.3 5.6 copy-start.39
  128.3 160.7 %all-to-all-start = ((bf16[3,16,8,72,128]{4,3,0,2,1:T(8,128)(2,1)}), bf16[3,16,8,72,128]{4,3,0,2,1:T(8,128)(2,1)}, u32[]{:S(2)}, u32[]{:S(2)}) async-start(bf16[3,16,8,72,128]{4,3,0,2,1:T(8,128)(2,1)} %copy.98), calls=%async_computation | async-start | bytes 14155776 | tf_op jit(solution)/shard_map/all_to_all | solution.py:131
  133.2 517.5 %all-gather.14.cloned.1.call-start = ((), (), s32[]{:S(2)}) async-start(), calls=%async_computation.12 | async-start | bytes 12533760 | tf_op jit(solution)/shard_map/all_gather | solution.py:159
  505.3 6.3 copy-start.40
  511.6 98.5 %all-to-all-start.1 = ((bf16[2,8,72,1024]{2,1,0,3:T(8,128)(2,1)}), bf16[2,8,72,1024]{2,1,0,3:T(8,128)(2,1)}, u32[]{:S(2)}, u32[]{:S(2)}) async-start(bf16[2,8,72,1024]{2,1,0,3:T(8,128)(2,1)} %bitcast.256), calls=%async_computation.1 | async-start | bytes 8388608 | tf_op jit(solution)/shard_map/all_to_all | solution.py:141
  516.2 879.1 %reduce-scatter.10.cloned.1.call-start = ((), (), s32[]{:S(2)}) async-start(), calls=%async_computation.14 | async-start | bytes 3317760 | tf_op jit(solution)/shard_map/reduce_scatter | solution.py:263
  625.9 57.4 %slice-start = ((s8[4718592]{0:T(1024)(128)(4,1)}), s8[524288]{0:T(1024)(128)(4,1)S(1)}, s32[]{:S(2)}) async-start(s8[4718592]{0:T(1024)(128)(4,1)} %bitcast.254), calls=%async_computation.20 | async-start | bytes 1048576
  650.7 32.6 %slice-start.1 = ((s8[4718592]{0:T(1024)(128)(4,1)}), s8[4194304]{0:T(1024)(128)(4,1)S(1)}, s32[]{:S(2)}) async-start(s8[4718592]{0:T(1024)(128)(4,1)} %bitcast.254), calls=%async_computation.21 | async-start | bytes 8388608
  707.4 3.8 copy-start.8
  715.6 679.7 %reduce-scatter.12.cloned.1.call-start = ((), (), s32[]{:S(2)}) async-start(), calls=%async_computation.15 | async-start | bytes 12533760 | tf_op jit(solution)/shard_map/reduce_scatter | solution.py:275
  741.2 6.2 copy-start.7
  742.9 59.0 %all-to-all-start.2 = ((bf16[16,8,72,128]{3,2,1,0:T(8,128)(2,1)}), bf16[16,8,72,128]{3,2,1,0:T(8,128)(2,1)}, u32[]{:S(2)}, u32[]{:S(2)}) async-start(bf16[16,8,72,128]{3,2,1,0:T(8,128)(2,1)} %copy.105), calls=%async_computation.2 | async-start | bytes 4718592 | tf_op jit(solution)/shard_map/all_to_all | solution.py:206
  747.3 648.0 %reduce-scatter.14.cloned.1.call-start = ((), (), s32[]{:S(2)}) async-start(), calls=%async_computation.16 | async-start | bytes 12533760 | tf_op jit(solution)/shard_map/reduce_scatter | solution.py:281
  763.8 693.3 %reduce-scatter.8.cloned.1.call-start = ((), (), s32[]{:S(2)}) async-start(), calls=%async_computation.13 | async-start | bytes 9953280 | tf_op jit(solution)/shard_map/reduce_scatter | solution.py:257
  1335.0 15.4 copy-start.2
  1335.0 15.4 copy-start.14
  1335.0 15.4 copy-start.16
  1335.0 15.4 copy-start.20
  1335.0 15.4 copy-start.27
  1335.0 15.4 copy-start.42
  1375.9 150.9 %reduce-scatter.16.cloned.1.call-start = ((), (), s32[]{:S(2)}) async-start(), calls=%async_computation.18 | async-start | bytes 368640
  1393.8 64.6 %copy-start.38 = (bf16[288]{0:T(512)(128)(2,1)S(1)}, bf16[288]{0:T(512)(128)(2,1)}, u32[]{:S(2)}) copy-start(bf16[288]{0:T(512)(128)(2,1)} %param.33) | copy-start | bytes 1732
  1395.2 217.6 %all-reduce.20.cloned.1.call-start = ((), (), s32[]{:S(2)}) async-start(), calls=%async_computation.19 | async-start | bytes 11354112 | tf_op jit(solution)/shard_map/psum | solution.py:311
  1395.8 362.7 %all-gather.16.cloned.1.call-start = ((), (), s32[]{:S(2)}) async-start(), calls=%async_computation.17 | async-start | bytes 17915904 | tf_op jit(solution)/shard_map/all_gather | solution.py:290
  1460.5 4.2 slice-start.2
  1470.8 9.3 copy-start.22
  1480.0 4.3 copy-start.23
  1480.0 4.3 copy-start.24
  1480.1 4.3 copy-start.25
  1480.1 4.3 copy-start.28
  1480.1 4.3 copy-start.29
  1480.1 20.9 %copy-start.18 = (f32[8,128]{1,0:T(8,128)S(1)}, f32[8,128]{1,0:T(8,128)}, u32[]{:S(2)}) copy-start(f32[8,128]{1,0:T(8,128)} %copy-done.17) | copy-start | bytes 12292
  1612.8 4.5 copy-start.10
  (28 other events, 59.5 us)
Sparse Core Ops, SparseCore 0:
  9.9 86.9 all-gather.7
  98.8 39.7 all-gather.9
  140.4 101.0 all-gather.11
  243.3 101.0 all-gather.13
  715.8 38.3 reduce-scatter.9
  757.2 99.7 reduce-scatter.11
  860.2 99.7 reduce-scatter.13
  1376.0 81.0 reduce-scatter.7
  1460.5 24.4 reduce-scatter.15
  1487.4 125.3 all-reduce.19
  1614.4 144.0 all-gather.15
